TPU v7x, 32 devices: a whole 2x2x4 slice. The times are simulated.
32 devices in a mesh: rep: 4 (over y, core), row: 4 (over z), col: 2 (over x).
Axes of the slice: x: 2, y: 2, z: 4, core: 2. Of those that a mesh axis runs over, the one named last changes fastest.
Arguments:
- patches: bfloat16 [4096, 588], P(('rep', 'col')), may hold values from -20 to 20
- embed_weight: bfloat16 [588, 6144], P(None, 'row'), may hold values from -1 to 1
- embed_bias: float32 [6144], P('row'), may hold values from -3 to 3
- old_in: bfloat16 [64, 768, 1536], P(('row', 'col')), may hold values from -0.078125 to 0.078125
- old_out: bfloat16 [64, 1536, 768], P(('row', 'col')), may hold values from -0.0546875 to 0.0546875
- restore_id: int32 [1], replicated, may hold values from 0 to 47
- norm_gains: float32 [48, 6144], P(None, 'row'), may hold values from 0.1 to 1.9
- in_biases: float32 [48, 12288], P(None, 'col'), may hold values from -3 to 3
- out_biases: float32 [48, 6144], P(None, 'row'), may hold values from -3 to 3
- final_gain: float32 [6144], P('row'), may hold values from 0.1 to 1.9
- check_weight: bfloat16 [6144, 128], P('row'), may hold values from -0.078125 to 0.078125
Outputs:
- in_weight: bfloat16 [6144, 12288], P('row', 'col')
- out_weight: bfloat16 [12288, 6144], P('col', 'row')
- check_logits: float32 [4096, 128], P(('rep', 'col'))
All inputs are finite; a program needn't handle non-finite values.
Results may differ from a plain program's by a relative error of at most 0.0062.
Values may be sent and summed in bfloat16 or wider, within the bound.
A program may use at most 192 MiB of HBM per device.

v0:
```python
import jax
import jax.numpy as jnp
from jax import lax
from jax.sharding import PartitionSpec as P

EPSILON = 1e-06


def for_sending(shard):
    return jax.tree.map(lambda a: a.astype(jnp.bfloat16) if a.dtype == jnp.float32 else a, shard)


def partner(value, axis, bit):
    mask = 2**bit
    pairs = [(source, source ^ mask) for source in range(lax.axis_size(axis))]
    return lax.ppermute(value, axis, pairs)


def pick_rows(restore_id, param_table):
    selector = (
        jnp.arange(param_table.shape[0], dtype=jnp.int32)[None, :] == restore_id[:, None]
    ).astype(jnp.float32)
    return jnp.dot(selector, param_table, precision=lax.Precision.HIGHEST)[0]


def norm_rows(values, gain_row):
    feature_count = values.shape[1] * lax.axis_size("row")
    totals = lax.psum((jnp.sum(values, axis=1), jnp.sum(values * values, axis=1)), "row")
    average = totals[0][:, None] / feature_count
    spread = totals[1][:, None] / feature_count - average * average
    return ((values - average) * lax.rsqrt(spread + EPSILON) * gain_row).astype(jnp.bfloat16)


def move_halves(pieces, bit_total, device_index, exchange):
    for bit_number in range(bit_total):
        upper_side = device_index >> bit_number & 1 == 1
        outgoing = tuple(
            (jnp.where(upper_side, lower_part, upper_part) for lower_part, upper_part in pieces)
        )
        incoming = exchange(outgoing, bit_number)
        pieces = tuple(
            (
                (
                    jnp.where(upper_side, arrived, lower_part),
                    jnp.where(upper_side, upper_part, arrived),
                )
                for (lower_part, upper_part), arrived in zip(pieces, incoming)
            )
        )
    return pieces


def on_device(
    patches,
    embed_weight,
    embed_bias,
    old_in,
    old_out,
    restore_id,
    norm_gains,
    in_biases,
    out_biases,
    final_gain,
    check_weight,
):
    tiles_here, tile_rows, tile_cols = old_in.shape
    local_cols = tiles_here * tile_cols
    half_cols = local_cols // 2
    in_local = jnp.transpose(old_in, (1, 0, 2)).reshape(tile_rows, local_cols)
    out_local = old_out.reshape(local_cols, tile_rows)
    col_index = lax.axis_index("col")
    col_count = lax.axis_size("col")
    col_bits = col_count.bit_length() - 1
    pieces = (
        (in_local[:, :half_cols], in_local[:, half_cols:]),
        (out_local[:half_cols], out_local[half_cols:]),
    )
    pieces = move_halves(
        pieces,
        col_bits,
        col_index,
        lambda send_parts, bit_number: jax.tree.map(
            lambda part, own: part.astype(own.dtype),
            partner(for_sending(send_parts), "col", bit_number),
            send_parts,
        ),
    )
    in_pair, out_pair = pieces
    in_weight = jnp.concatenate(in_pair, axis=0)
    out_weight = jnp.concatenate(out_pair, axis=1)
    layer_gain = pick_rows(restore_id, norm_gains)
    in_bias = pick_rows(restore_id, in_biases)
    out_bias = pick_rows(restore_id, out_biases)
    embedded = jnp.dot(patches, embed_weight, preferred_element_type=jnp.float32) + embed_bias
    normed = norm_rows(embedded, layer_gain)
    partial_pre = jnp.dot(
        lax.all_gather(normed, "col", axis=0, tiled=True),
        in_weight,
        preferred_element_type=jnp.float32,
    )
    pre_share = lax.psum_scatter(partial_pre, "row", scatter_dimension=0, tiled=True) + in_bias
    hidden = jax.nn.gelu(pre_share, approximate=False).astype(jnp.bfloat16)
    partial_branch = jnp.dot(
        lax.all_gather(hidden, "row", axis=0, tiled=True),
        out_weight,
        preferred_element_type=jnp.float32,
    )
    updated = (
        embedded
        + lax.psum_scatter(partial_branch, "col", scatter_dimension=0, tiled=True)
        + out_bias
    )
    final_normed = norm_rows(updated, final_gain)
    check_logits = lax.psum(
        jnp.dot(final_normed, check_weight, preferred_element_type=jnp.float32), "row"
    )
    return (in_weight, out_weight, check_logits)


def solution(mesh):
    placed = (
        P(("rep", "col"), None),
        P(None, "row"),
        P("row"),
        P(("row", "col"), None, None),
        P(("row", "col"), None, None),
        P(),
        P(None, "row"),
        P(None, "col"),
        P(None, "row"),
        P("row"),
        P("row", None),
    )
    return jax.shard_map(
        on_device,
        mesh=mesh,
        in_specs=placed,
        out_specs=(P("row", "col"), P("col", "row"), P(("rep", "col"), None)),
        check_vma=False,
    )
```

profile of v0, /device:TPU:0, one launch (start us, length us, event | category | flops | bytes accessed | tf_op | source)
XLA Modules:
  0.0 1160.1 jit_solution(9391864358575194546)
XLA Ops:
  7.2 0.0 copy-start
  7.2 0.0 all-gather.3.cloned.1.call-start
  7.2 10.0 copy.15
  17.2 0.0 copy-start.2
  17.2 0.0 copy-start.8
  17.2 0.0 copy-start.9
  17.2 4.0 broadcast_select_fusion.2
  21.3 5.6 copy-done.2
  26.9 3.0 collective-permute-start
  30.5 3.2 fusion.22
  33.7 11.9 %all-reduce.1 = (f32[512]{0:T(512)S(1)}, f32[512]{0:T(512)S(1)}) all-reduce(f32[512]{0:T(512)S(1)} %get-tuple-element.6, f32[512]{0:T(512)S(1)} %get-tuple-element.5), channel_id=1, replica_groups=mesh['rep'=4,'row'=4,'col'=2] {'row'}, use_global_device_ids=true, to_apply=%region_3.4 | all-reduce | flops 1024 | bytes 8192 | tf_op jit(solution)/shard_map/psum | solution.py:28
  45.7 0.2 convolution_reduce_fusion.1
  45.9 3.6 multiply_convert_fusion.1
  49.5 0.0 all-gather.3.cloned.1.call-update
  49.5 0.0 reduce-scatter.3.cloned.1.call-start
  49.6 217.2 %collective-permute-done = bf16[768,6144]{1,0:T(8,128)(2,1)} collective-permute-done((bf16[768,6144]{1,0:T(8,128)(2,1)}, bf16[768,6144]{1,0:T(8,128)(2,1)}, u32[]{:S(2)}, u32[]{:S(2)}) %collective-permute-start) | collective-permute-done | bytes 9437216 | tf_op jit(solution)/shard_map/ppermute | solution.py:16
  266.8 9.7 broadcast_select_fusion.1
  276.5 21.6 %pad_maximum_fusion = bf16[1536,6144]{1,0:T(8,128)(2,1)} fusion(bf16[768,6144]{1,0:T(8,128)(2,1)S(1)} %get-tuple-element.13, bf16[768,6144]{1,0:T(8,128)(2,1)S(1)} %get-tuple-element.12), kind=kLoop, calls=%fused_computation | loop fusion | flops 37748736 | bytes 37748736 | tf_op jit(solution)/shard_map/concatenate | solution.py:89
  298.1 26.1 %fusion.24 = f32[1024,6144]{1,0:T(8,128)} fusion(bf16[1024,1536]{1,0:T(8,128)(2,1)} %all-gather.3.cloned.1.call-done, bf16[1536,6144]{1,0:T(8,128)(2,1)} %pad_maximum_fusion), kind=kOutput, calls=%fused_computation.54 | convolution fusion | flops 19327352832 | bytes 47185920 | tf_op jit(solution)/shard_map/dot_general | solution.py:96
  324.3 0.0 reduce-scatter.3.cloned.1.call-update
  324.3 0.0 all-gather.5.cloned.1.call-start
  324.3 1.2 copy-done.3
  325.5 0.5 fusion.15
  326.0 414.1 %reduce-scatter.3.cloned.1.call-done = f32[256,6144]{1,0:T(8,128)} async-done(((f32[1024,6144]{1,0:T(8,128)}), f32[256,6144]{1,0:T(8,128)}) %reduce-scatter.3.cloned.1.call-update) | async-done | bytes 6291472 | tf_op jit(solution)/shard_map/reduce_scatter | solution.py:101
  740.1 15.9 %fusion.2 = bf16[256,6144]{1,0:T(8,128)(2,1)} fusion(f32[256,6144]{1,0:T(8,128)} %reduce-scatter.3.cloned.1.call-done, f32[6144]{0:T(1024)S(1)} %bitcast.36), kind=kLoop, calls=%fused_computation.11 | loop fusion | flops 103809024 | bytes 9461760 | tf_op jit(solution)/shard_map/convert_element_type | solution.py:102
  756.0 0.0 all-gather.5.cloned.1.call-update
  756.0 0.2 reduce-scatter.5.cloned.1.call-start
  756.3 7.5 fusion.23
  763.8 1.1 bitcast_select_fusion.1
  764.8 1.5 collective-permute-start.1
  766.4 203.3 %collective-permute-done.1 = bf16[6144,768]{1,0:T(8,128)(2,1)} collective-permute-done((bf16[6144,768]{1,0:T(8,128)(2,1)S(1)}, bf16[6144,768]{1,0:T(8,128)(2,1)}, u32[]{:S(2)}, u32[]{:S(2)}) %collective-permute-start.1) | collective-permute-done | bytes 9437216 | tf_op jit(solution)/shard_map/ppermute | solution.py:16
  969.7 9.6 bitcast_select_fusion.2
  979.3 14.5 %pad_maximum_fusion.1 = bf16[6144,1536]{1,0:T(8,128)(2,1)} fusion(bf16[6144,768]{1,0:T(8,128)(2,1)} %get-tuple-element.17, bf16[6144,768]{1,0:T(8,128)(2,1)S(1)} %get-tuple-element.16), kind=kLoop, calls=%fused_computation.1 | loop fusion | flops 37748736 | bytes 37748736 | tf_op jit(solution)/shard_map/concatenate | solution.py:90
  993.8 26.1 %fusion.25 = f32[1024,1536]{1,0:T(8,128)} fusion(bf16[1024,6144]{1,0:T(8,128)(2,1)} %all-gather.5.cloned.1.call-done, bf16[6144,1536]{1,0:T(8,128)(2,1)} %pad_maximum_fusion.1), kind=kOutput, calls=%fused_computation.55 | convolution fusion | flops 19327352832 | bytes 37748736 | tf_op jit(solution)/shard_map/dot_general | solution.py:103
  1019.9 0.0 reduce-scatter.5.cloned.1.call-update
  1020.0 0.0 copy-start.4
  1020.0 0.0 copy-start.7
  1020.0 0.0 all-reduce.4.cloned.1.call-start
  1020.0 0.9 copy-done.6
  1020.9 0.2 convolution_reduce_fusion
  1021.1 78.1 %reduce-scatter.5.cloned.1.call-done = f32[512,1536]{1,0:T(8,128)} async-done(((f32[1024,1536]{1,0:T(8,128)}), f32[512,1536]{1,0:T(8,128)}) %reduce-scatter.5.cloned.1.call-update) | async-done | bytes 3145744 | tf_op jit(solution)/shard_map/reduce_scatter | solution.py:110
  1099.2 4.8 fusion.21
  1104.0 11.7 %all-reduce = (f32[512]{0:T(512)S(1)}, f32[512]{0:T(512)S(1)}) all-reduce(f32[512]{0:T(512)S(1)} %get-tuple-element.4, f32[512]{0:T(512)S(1)} %get-tuple-element.3), channel_id=1, replica_groups=mesh['rep'=4,'row'=4,'col'=2] {'row'}, use_global_device_ids=true, to_apply=%region_9.10 | all-reduce | flops 1024 | bytes 8192 | tf_op jit(solution)/shard_map/psum | solution.py:28
  1115.7 3.2 fusion.10
  1118.9 0.0 all-reduce.4.cloned.1.call-update
  1119.0 33.0 %all-reduce.4.cloned.1.call-done = f32[512,128]{1,0:T(8,128)} async-done(((f32[512,128]{1,0:T(8,128)}), f32[512,128]{1,0:T(8,128)}) %all-reduce.4.cloned.1.call-update) | async-done | bytes 262160 | tf_op jit(solution)/shard_map/psum | solution.py:114
  1151.9 1.7 copy.18
  1153.6 0.0 copy-done.1
  (14 shorter events, 0.0 us)
Async XLA Ops:
  7.2 23.3 %copy-start = (bf16[588,1536]{1,0:T(8,128)(2,1)S(1)}, bf16[588,1536]{1,0:T(8,128)(2,1)}, u32[]{:S(2)}) copy-start(bf16[588,1536]{1,0:T(8,128)(2,1)} %param.12) | copy-start | bytes 5419012
  7.2 291.0 %all-gather.3.cloned.1.call-start = ((), (), s32[]{:S(2)}) async-start(), calls=%async_computation.2 | async-start | bytes 4718592 | tf_op jit(solution)/shard_map/all_gather | solution.py:97
  17.2 9.7 copy-start.2
  17.2 13.3 %copy-start.8 = (bf16[512,588]{0,1:T(8,128)(2,1)S(1)}, bf16[512,588]{0,1:T(8,128)(2,1)}, u32[]{:S(2)}) copy-start(bf16[512,588]{0,1:T(8,128)(2,1)} %param.11) | copy-start | bytes 1806340
  17.2 13.3 %copy-start.9 = (f32[1536]{0:T(1024)S(1)}, f32[1536]{0:T(1024)}, u32[]{:S(2)}) copy-start(f32[1536]{0:T(1024)} %param.13) | copy-start | bytes 18436
  26.9 18.8 %copy-start.5 = (f32[48,1536]{1,0:T(8,128)S(1)}, f32[48,1536]{1,0:T(8,128)}, u32[]{:S(2)}) copy-start(f32[48,1536]{1,0:T(8,128)} %param.17) | copy-start | bytes 884740
  26.9 239.9 %collective-permute-start = (bf16[768,6144]{1,0:T(8,128)(2,1)}, bf16[768,6144]{1,0:T(8,128)(2,1)}, u32[]{:S(2)}, u32[]{:S(2)}) collective-permute-start(bf16[768,6144]{1,0:T(8,128)(2,1)} %broadcast_select_fusion.2), channel_id=1, source_target_pairs={{0,1},{1,0},{2,3},{3,2},{4,5},{5,4},{6,7},{7,6},{8,9},{9,8},{10,11... | collective-permute-start | bytes 28311560 | tf_op jit(solution)/shard_map/ppermute | solution.py:16
  49.5 690.6 %reduce-scatter.3.cloned.1.call-start = ((), (), s32[]{:S(2)}) async-start(), calls=%async_computation.3 | async-start | bytes 31457280 | tf_op jit(solution)/shard_map/reduce_scatter | solution.py:101
  324.3 1.3 copy-start.3
  324.3 669.5 %all-gather.5.cloned.1.call-start = ((), (), s32[]{:S(2)}) async-start(), calls=%async_computation.4 | async-start | bytes 15728640 | tf_op jit(solution)/shard_map/all_gather | solution.py:104
  756.0 343.1 %reduce-scatter.5.cloned.1.call-start = ((), (), s32[]{:S(2)}) async-start(), calls=%async_computation.5 | async-start | bytes 9437184 | tf_op jit(solution)/shard_map/reduce_scatter | solution.py:110
  764.8 204.9 %collective-permute-start.1 = (bf16[6144,768]{1,0:T(8,128)(2,1)S(1)}, bf16[6144,768]{1,0:T(8,128)(2,1)}, u32[]{:S(2)}, u32[]{:S(2)}) collective-permute-start(bf16[6144,768]{1,0:T(8,128)(2,1)S(1)} %bitcast_select_fusion.1), channel_id=1, source_target_pairs={{0,1},{1,0},{2,3},{3,2},{4,5},{5,4},{6,7},{7,6},{8,9},{9,8},{10,11... | collective-permute-start | bytes 28311560 | tf_op jit(solution)/shard_map/ppermute | solution.py:16
  1019.9 1.0 copy-start.6
  1020.0 95.8 %copy-start.4 = (bf16[1536,128]{1,0:T(8,128)(2,1)S(1)}, bf16[1536,128]{1,0:T(8,128)(2,1)}, u32[]{:S(2)}) copy-start(bf16[1536,128]{1,0:T(8,128)(2,1)} %param.21) | copy-start | bytes 1179652
  1020.0 95.7 %copy-start.7 = (f32[1536]{0:T(1024)S(1)}, f32[1536]{0:T(1024)}, u32[]{:S(2)}) copy-start(f32[1536]{0:T(1024)} %param.20) | copy-start | bytes 18436
  1020.0 132.0 %all-reduce.4.cloned.1.call-start = ((), (), s32[]{:S(2)}) async-start(), calls=%async_computation.6 | async-start | bytes 524288 | tf_op jit(solution)/shard_map/psum | solution.py:114
  1020.9 132.7 %copy-start.1 = (bf16[588,1536]{1,0:T(8,128)(2,1)S(1)}, bf16[588,1536]{1,0:T(8,128)(2,1)}, u32[]{:S(2)}) copy-start(bf16[588,1536]{1,0:T(8,128)(2,1)} %param.12) | copy-start | bytes 5419012
Sparse Core Ops, SparseCore 0:
  49.6 75.9 all-gather.2
  324.4 415.6 reduce-scatter.2
  756.2 220.1 all-gather.4
  1020.1 79.0 reduce-scatter.4
  1119.1 32.8 all-reduce.3
where the time goes:
time: 1160 us
  waiting for transfers between devices  946 us (82%)
  other arithmetic  84.8 us (7%)
  matrix products  59.6 us (5%)
  local copies, waits for them, and re-layouts  26.9 us (2%)
  blocking collectives  23.6 us (2%)
  between operations  14.6 us (1%)
    ppermute x2, waiting for transfers between devices, partner(): return lax.ppermute(value, axis, pairs)  421 us
    reduce_scatter x1, waiting for transfers between devices, on_device(): lax.psum_scatter(partial_pre, 'row', scatter_dimension=0, tiled=True)  414 us
    reduce_scatter x1, waiting for transfers between devices, on_device(): lax.psum_scatter(partial_branch, 'col', scatter_dimension=0, tiled=True)  78.1 us
    psum x1, waiting for transfers between devices, on_device(): lax.psum(jnp.dot(final_normed, check_weight, preferred_element_type=jnp.f...  33 us
    dot_general x1, matrix products, on_device(): jnp.dot(lax.all_gather(hidden, 'row', axis=0, tiled=True), out_weight, pr...  26.1 us
    dot_general x1, matrix products, on_device(): jnp.dot(lax.all_gather(normed, 'col', axis=0, tiled=True), in_weight, pre...  26.1 us
    psum x2, blocking collectives, norm_rows(): lax.psum((jnp.sum(values, axis=1), jnp.sum(values * values, axis=1)), 'row')  23.6 us
  transfers between devices with their start and end apart: 7, of which 5 were waited for; matrix products, arithmetic and copies ran while one was open for 6% of the time, Pallas kernels for 0%

commit v1 on v0

--- a/solution.py
+++ b/solution.py
@@ -111,8 +111,11 @@
         + out_bias
     )
     final_normed = norm_rows(updated, final_gain)
-    check_logits = lax.psum(
-        jnp.dot(final_normed, check_weight, preferred_element_type=jnp.float32), "row"
+    check_logits = jnp.sum(
+        lax.all_gather(
+            jnp.dot(final_normed, check_weight, preferred_element_type=jnp.float32), "row"
+        ),
+        axis=0,
     )
     return (in_weight, out_weight, check_logits)
 

time: 1160 us -> 1150 us (level)
    psum x1 -> x0, waiting for transfers between devices: 33 us -> none  [on_device(): lax.psum(jnp.dot(final_normed, check_weight, preferred_element_type=jnp.f...]
    all_gather x0 -> x1, waiting for transfers between devices: none -> 25.4 us  [on_device(): lax.all_gather(jnp.dot(final_normed, check_weight, preferred_element_type...]
where the time goes in v1:
time: 1150 us
  waiting for transfers between devices  938 us (82%)
  other arithmetic  86.8 us (8%)
  matrix products  59.6 us (5%)
  local copies, waits for them, and re-layouts  25.2 us (2%)
  blocking collectives  23.6 us (2%)
  between operations  14.6 us (1%)
    ppermute x2, waiting for transfers between devices, partner(): return lax.ppermute(value, axis, pairs)  421 us
    reduce_scatter x1, waiting for transfers between devices, on_device(): lax.psum_scatter(partial_pre, 'row', scatter_dimension=0, tiled=True)  414 us
    reduce_scatter x1, waiting for transfers between devices, on_device(): lax.psum_scatter(partial_branch, 'col', scatter_dimension=0, tiled=True)  78.1 us
    dot_general x1, matrix products, on_device(): jnp.dot(lax.all_gather(hidden, 'row', axis=0, tiled=True), out_weight, pr...  26.1 us
    dot_general x1, matrix products, on_device(): jnp.dot(lax.all_gather(normed, 'col', axis=0, tiled=True), in_weight, pre...  26.1 us
    all_gather x1, waiting for transfers between devices, on_device(): lax.all_gather(jnp.dot(final_normed, check_weight, preferred_element_type...  25.4 us
    psum x2, blocking collectives, norm_rows(): lax.psum((jnp.sum(values, axis=1), jnp.sum(values * values, axis=1)), 'row')  23.6 us
  transfers between devices with their start and end apart: 7, of which 5 were waited for; matrix products, arithmetic and copies ran while one was open for 6% of the time, Pallas kernels for 0%

profile of v1, /device:TPU:0, one launch (start us, length us, event | category | flops | bytes accessed | tf_op | source)
XLA Modules:
  0.0 1152.9 jit_solution(8650716443930202391)
XLA Ops:
  7.2 0.0 copy-start
  7.2 0.0 all-gather.5.cloned.1.call-start
  7.2 10.0 copy.15
  17.2 0.0 copy-start.2
  17.2 0.0 copy-start.8
  17.2 0.0 copy-start.9
  17.2 4.0 broadcast_select_fusion.2
  21.3 5.6 copy-done.2
  26.9 3.0 collective-permute-start
  30.5 0.0 copy-done
  30.5 3.2 fusion.22
  33.7 11.9 %all-reduce.1 = (f32[512]{0:T(512)S(1)}, f32[512]{0:T(512)S(1)}) all-reduce(f32[512]{0:T(512)S(1)} %get-tuple-element.6, f32[512]{0:T(512)S(1)} %get-tuple-element.5), channel_id=1, replica_groups=mesh['rep'=4,'row'=4,'col'=2] {'row'}, use_global_device_ids=true, to_apply=%region_3.4 | all-reduce | flops 1024 | bytes 8192 | tf_op jit(solution)/shard_map/psum | solution.py:28
  45.7 0.2 convolution_reduce_fusion.1
  45.9 3.6 multiply_convert_fusion.1
  49.5 0.0 all-gather.5.cloned.1.call-update
  49.5 0.0 reduce-scatter.3.cloned.1.call-start
  49.6 217.2 %collective-permute-done = bf16[768,6144]{1,0:T(8,128)(2,1)} collective-permute-done((bf16[768,6144]{1,0:T(8,128)(2,1)}, bf16[768,6144]{1,0:T(8,128)(2,1)}, u32[]{:S(2)}, u32[]{:S(2)}) %collective-permute-start) | collective-permute-done | bytes 9437216 | tf_op jit(solution)/shard_map/ppermute | solution.py:16
  266.8 9.7 broadcast_select_fusion.1
  276.5 21.6 %pad_maximum_fusion = bf16[1536,6144]{1,0:T(8,128)(2,1)} fusion(bf16[768,6144]{1,0:T(8,128)(2,1)S(1)} %get-tuple-element.13, bf16[768,6144]{1,0:T(8,128)(2,1)S(1)} %get-tuple-element.12), kind=kLoop, calls=%fused_computation | loop fusion | flops 37748736 | bytes 37748736 | tf_op jit(solution)/shard_map/concatenate | solution.py:89
  298.1 26.1 %fusion.24 = f32[1024,6144]{1,0:T(8,128)} fusion(bf16[1024,1536]{1,0:T(8,128)(2,1)} %all-gather.5.cloned.1.call-done, bf16[1536,6144]{1,0:T(8,128)(2,1)} %pad_maximum_fusion), kind=kOutput, calls=%fused_computation.54 | convolution fusion | flops 19327352832 | bytes 47185920 | tf_op jit(solution)/shard_map/dot_general | solution.py:96
  324.3 0.0 reduce-scatter.3.cloned.1.call-update
  324.3 0.0 all-gather.7.cloned.1.call-start
  324.3 1.2 copy-done.3
  325.5 0.5 fusion.15
  326.0 414.1 %reduce-scatter.3.cloned.1.call-done = f32[256,6144]{1,0:T(8,128)} async-done(((f32[1024,6144]{1,0:T(8,128)}), f32[256,6144]{1,0:T(8,128)}) %reduce-scatter.3.cloned.1.call-update) | async-done | bytes 6291472 | tf_op jit(solution)/shard_map/reduce_scatter | solution.py:101
  740.1 15.9 %fusion.2 = bf16[256,6144]{1,0:T(8,128)(2,1)} fusion(f32[256,6144]{1,0:T(8,128)} %reduce-scatter.3.cloned.1.call-done, f32[6144]{0:T(1024)S(1)} %bitcast.38), kind=kLoop, calls=%fused_computation.11 | loop fusion | flops 103809024 | bytes 9461760 | tf_op jit(solution)/shard_map/convert_element_type | solution.py:102
  756.0 0.0 all-gather.7.cloned.1.call-update
  756.0 0.2 reduce-scatter.5.cloned.1.call-start
  756.3 7.5 fusion.23
  763.8 1.1 bitcast_select_fusion.1
  764.8 1.5 collective-permute-start.1
  766.4 203.3 %collective-permute-done.1 = bf16[6144,768]{1,0:T(8,128)(2,1)} collective-permute-done((bf16[6144,768]{1,0:T(8,128)(2,1)S(1)}, bf16[6144,768]{1,0:T(8,128)(2,1)}, u32[]{:S(2)}, u32[]{:S(2)}) %collective-permute-start.1) | collective-permute-done | bytes 9437216 | tf_op jit(solution)/shard_map/ppermute | solution.py:16
  969.7 9.6 bitcast_select_fusion.2
  979.3 14.5 %pad_maximum_fusion.1 = bf16[6144,1536]{1,0:T(8,128)(2,1)} fusion(bf16[6144,768]{1,0:T(8,128)(2,1)} %get-tuple-element.17, bf16[6144,768]{1,0:T(8,128)(2,1)S(1)} %get-tuple-element.16), kind=kLoop, calls=%fused_computation.1 | loop fusion | flops 37748736 | bytes 37748736 | tf_op jit(solution)/shard_map/concatenate | solution.py:90
  993.8 26.1 %fusion.25 = f32[1024,1536]{1,0:T(8,128)} fusion(bf16[1024,6144]{1,0:T(8,128)(2,1)} %all-gather.7.cloned.1.call-done, bf16[6144,1536]{1,0:T(8,128)(2,1)} %pad_maximum_fusion.1), kind=kOutput, calls=%fused_computation.55 | convolution fusion | flops 19327352832 | bytes 37748736 | tf_op jit(solution)/shard_map/dot_general | solution.py:103
  1019.9 0.0 reduce-scatter.5.cloned.1.call-update
  1020.0 0.0 copy-start.4
  1020.0 0.0 copy-start.7
  1020.0 0.0 all-gather.9.cloned.1.call-start
  1020.0 0.9 copy-done.6
  1020.9 0.2 convolution_reduce_fusion
  1021.1 78.1 %reduce-scatter.5.cloned.1.call-done = f32[512,1536]{1,0:T(8,128)} async-done(((f32[1024,1536]{1,0:T(8,128)}), f32[512,1536]{1,0:T(8,128)}) %reduce-scatter.5.cloned.1.call-update) | async-done | bytes 3145744 | tf_op jit(solution)/shard_map/reduce_scatter | solution.py:110
  1099.2 4.8 fusion.21
  1104.0 11.7 %all-reduce = (f32[512]{0:T(512)S(1)}, f32[512]{0:T(512)S(1)}) all-reduce(f32[512]{0:T(512)S(1)} %get-tuple-element.4, f32[512]{0:T(512)S(1)} %get-tuple-element.3), channel_id=1, replica_groups=mesh['rep'=4,'row'=4,'col'=2] {'row'}, use_global_device_ids=true, to_apply=%region_9.10 | all-reduce | flops 1024 | bytes 8192 | tf_op jit(solution)/shard_map/psum | solution.py:28
  1115.7 3.2 fusion.10
  1118.9 0.0 all-gather.9.cloned.1.call-update
  1119.0 25.4 %all-gather.9.cloned.1.call-done = f32[2048,128]{1,0:T(8,128)} async-done(((f32[512,128]{1,0:T(8,128)}), f32[2048,128]{1,0:T(8,128)}) %all-gather.9.cloned.1.call-update) | async-done | bytes 1048592 | tf_op jit(solution)/shard_map/all_gather | solution.py:115
  1144.3 2.0 reduce_sum.49
  (14 shorter events, 0.0 us)
Async XLA Ops:
  7.2 23.3 %copy-start = (bf16[588,1536]{1,0:T(8,128)(2,1)S(1)}, bf16[588,1536]{1,0:T(8,128)(2,1)}, u32[]{:S(2)}) copy-start(bf16[588,1536]{1,0:T(8,128)(2,1)} %param.12) | copy-start | bytes 5419012
  7.2 291.0 %all-gather.5.cloned.1.call-start = ((), (), s32[]{:S(2)}) async-start(), calls=%async_computation.2 | async-start | bytes 4718592 | tf_op jit(solution)/shard_map/all_gather | solution.py:97
  17.2 9.7 copy-start.2
  17.2 13.3 %copy-start.8 = (bf16[512,588]{0,1:T(8,128)(2,1)S(1)}, bf16[512,588]{0,1:T(8,128)(2,1)}, u32[]{:S(2)}) copy-start(bf16[512,588]{0,1:T(8,128)(2,1)} %param.11) | copy-start | bytes 1806340
  17.2 13.3 %copy-start.9 = (f32[1536]{0:T(1024)S(1)}, f32[1536]{0:T(1024)}, u32[]{:S(2)}) copy-start(f32[1536]{0:T(1024)} %param.13) | copy-start | bytes 18436
  26.9 18.8 %copy-start.5 = (f32[48,1536]{1,0:T(8,128)S(1)}, f32[48,1536]{1,0:T(8,128)}, u32[]{:S(2)}) copy-start(f32[48,1536]{1,0:T(8,128)} %param.17) | copy-start | bytes 884740
  26.9 239.9 %collective-permute-start = (bf16[768,6144]{1,0:T(8,128)(2,1)}, bf16[768,6144]{1,0:T(8,128)(2,1)}, u32[]{:S(2)}, u32[]{:S(2)}) collective-permute-start(bf16[768,6144]{1,0:T(8,128)(2,1)} %broadcast_select_fusion.2), channel_id=1, source_target_pairs={{0,1},{1,0},{2,3},{3,2},{4,5},{5,4},{6,7},{7,6},{8,9},{9,8},{10,11... | collective-permute-start | bytes 28311560 | tf_op jit(solution)/shard_map/ppermute | solution.py:16
  49.5 690.6 %reduce-scatter.3.cloned.1.call-start = ((), (), s32[]{:S(2)}) async-start(), calls=%async_computation.3 | async-start | bytes 31457280 | tf_op jit(solution)/shard_map/reduce_scatter | solution.py:101
  324.3 1.3 copy-start.3
  324.3 669.5 %all-gather.7.cloned.1.call-start = ((), (), s32[]{:S(2)}) async-start(), calls=%async_computation.4 | async-start | bytes 15728640 | tf_op jit(solution)/shard_map/all_gather | solution.py:104
  756.0 343.1 %reduce-scatter.5.cloned.1.call-start = ((), (), s32[]{:S(2)}) async-start(), calls=%async_computation.5 | async-start | bytes 9437184 | tf_op jit(solution)/shard_map/reduce_scatter | solution.py:110
  764.8 204.9 %collective-permute-start.1 = (bf16[6144,768]{1,0:T(8,128)(2,1)S(1)}, bf16[6144,768]{1,0:T(8,128)(2,1)}, u32[]{:S(2)}, u32[]{:S(2)}) collective-permute-start(bf16[6144,768]{1,0:T(8,128)(2,1)S(1)} %bitcast_select_fusion.1), channel_id=1, source_target_pairs={{0,1},{1,0},{2,3},{3,2},{4,5},{5,4},{6,7},{7,6},{8,9},{9,8},{10,11... | collective-permute-start | bytes 28311560 | tf_op jit(solution)/shard_map/ppermute | solution.py:16
  1019.9 1.0 copy-start.6
  1020.0 95.8 %copy-start.4 = (bf16[1536,128]{1,0:T(8,128)(2,1)S(1)}, bf16[1536,128]{1,0:T(8,128)(2,1)}, u32[]{:S(2)}) copy-start(bf16[1536,128]{1,0:T(8,128)(2,1)} %param.21) | copy-start | bytes 1179652
  1020.0 95.7 %copy-start.7 = (f32[1536]{0:T(1024)S(1)}, f32[1536]{0:T(1024)}, u32[]{:S(2)}) copy-start(f32[1536]{0:T(1024)} %param.20) | copy-start | bytes 18436
  1020.0 124.3 %all-gather.9.cloned.1.call-start = ((), (), s32[]{:S(2)}) async-start(), calls=%async_computation.6 | async-start | bytes 1310720 | tf_op jit(solution)/shard_map/all_gather | solution.py:115
  1020.9 125.4 %copy-start.1 = (bf16[588,1536]{1,0:T(8,128)(2,1)S(1)}, bf16[588,1536]{1,0:T(8,128)(2,1)}, u32[]{:S(2)}) copy-start(bf16[588,1536]{1,0:T(8,128)(2,1)} %param.12) | copy-start | bytes 5419012
Sparse Core Ops, SparseCore 0:
  49.6 75.9 all-gather.4
  324.4 415.6 reduce-scatter.2
  756.2 220.1 all-gather.6
  1020.1 79.0 reduce-scatter.4
  1119.1 25.2 all-gather.8
